TPU v7x, 32 devices: a whole 2x2x4 slice. The times are simulated.
32 devices in a mesh: wide: 8 (over z, x), group: 4 (over y, core).
Axes of the slice: x: 2, y: 2, z: 4, core: 2. Of those that a mesh axis runs over, the one named last changes fastest.
Arguments:
- feat4: bfloat16 [32, 24, 24, 256], P(('wide', 'group')), may hold values from -100 to 100
- feat5: bfloat16 [32, 12, 12, 256], P(('wide', 'group')), may hold values from -100 to 100
- feat6: bfloat16 [32, 6, 6, 256], P(('wide', 'group')), may hold values from -100 to 100
- feat7: bfloat16 [32, 3, 3, 256], P(('wide', 'group')), may hold values from -100 to 100
- out_grad4: bfloat16 [32, 24, 24, 256], P(('wide', 'group')), may hold values from -6 to 6
- out_grad5: bfloat16 [32, 12, 12, 256], P(('wide', 'group')), may hold values from -6 to 6
- out_grad6: bfloat16 [32, 6, 6, 256], P(('wide', 'group')), may hold values from -6 to 6
- out_grad7: bfloat16 [32, 3, 3, 256], P(('wide', 'group')), may hold values from -6 to 6
- conv_weight: bfloat16 [3, 3, 256, 256], replicated, may hold values from -0.125 to 0.125
- bn_gain: float32 [4, 256], replicated, may hold values from 0.25 to 1.75
- bn_shift: float32 [4, 256], replicated, may hold values from -0.5 to 0.5
- heights: int32 [32], P(('wide', 'group')), may hold values from 168 to 384
- widths: int32 [32], P(('wide', 'group')), may hold values from 168 to 384
Outputs:
- out4: bfloat16 [32, 24, 24, 256], P(('wide', 'group'))
- out5: bfloat16 [32, 12, 12, 256], P(('wide', 'group'))
- out6: bfloat16 [32, 6, 6, 256], P(('wide', 'group'))
- out7: bfloat16 [32, 3, 3, 256], P(('wide', 'group'))
- d_feat4: bfloat16 [32, 24, 24, 256], P(('wide', 'group'))
- d_feat5: bfloat16 [32, 12, 12, 256], P(('wide', 'group'))
- d_feat6: bfloat16 [32, 6, 6, 256], P(('wide', 'group'))
- d_feat7: bfloat16 [32, 3, 3, 256], P(('wide', 'group'))
- d_weight: float32 [3, 3, 256, 256], replicated
- d_gain: float32 [4, 256], replicated
- d_shift: float32 [4, 256], replicated
Inputs may be any that keep to these rules, and one draw needn't show every extreme that they name: `heights`: pixel height of the valid part of each image. `widths`: pixel width of the valid part of each image.
All inputs are finite; a program needn't handle non-finite values.
Results may differ from a plain program's by a relative error of at most 0.0049.
Values sent between devices are 32-bit elements; how exact they have to be, the bound alone decides.
No kernel may reach another device: no remote copies, remote signals or barrier semaphores. Data moves between devices by JAX's collectives and lax.ppermute only.
A program may use at most 64 MiB of HBM per device.

v0:
```python
import jax
import jax.numpy as jnp
from jax import lax
from jax.sharding import PartitionSpec as P

EPSILON = 1e-05


def level_mask(heights, widths, stride, extent):
    row_limit = (heights[0] + stride - 1) // stride
    col_limit = (widths[0] + stride - 1) // stride
    row_place = lax.broadcasted_iota(jnp.int32, (extent, extent), 0)
    col_place = lax.broadcasted_iota(jnp.int32, (extent, extent), 1)
    inside = jnp.logical_and(row_place < row_limit, col_place < col_limit)
    return (inside.astype(jnp.float32), row_limit)


def conv_rows(padded, conv_weight, start_row, row_count, extent):
    summed = jnp.zeros((row_count * extent, conv_weight.shape[3]), jnp.float32)
    for tap_row in range(3):
        for tap_col in range(3):
            window = lax.dynamic_slice_in_dim(padded, start_row + tap_row, row_count, 0)[
                :, tap_col : tap_col + extent, :
            ]
            summed = summed + jnp.dot(
                window.reshape(row_count * extent, -1),
                conv_weight[tap_row, tap_col],
                preferred_element_type=jnp.float32,
            )
    return summed.reshape(row_count, extent, -1)


def input_grad_rows(padded_back, conv_weight, start_row, row_count, extent):
    summed = jnp.zeros((row_count * extent, conv_weight.shape[2]), jnp.float32)
    for tap_row in range(3):
        for tap_col in range(3):
            window = lax.dynamic_slice_in_dim(padded_back, start_row + 2 - tap_row, row_count, 0)[
                :, 2 - tap_col : 2 - tap_col + extent, :
            ]
            summed = summed + lax.dot_general(
                window.reshape(row_count * extent, -1),
                conv_weight[tap_row, tap_col],
                (((1,), (1,)), ((), ())),
                preferred_element_type=jnp.float32,
            )
    return summed.reshape(row_count, extent, -1)


def weight_grad_rows(padded, back_rows, start_row, row_count, extent):
    flat_back = back_rows.reshape(row_count * extent, -1)
    tap_terms = []
    for tap_row in range(3):
        for tap_col in range(3):
            window = lax.dynamic_slice_in_dim(padded, start_row + tap_row, row_count, 0)[
                :, tap_col : tap_col + extent, :
            ]
            tap_terms.append(
                lax.dot_general(
                    window.reshape(row_count * extent, -1),
                    flat_back,
                    (((0,), (0,)), ((), ())),
                    preferred_element_type=jnp.float32,
                )
            )
    return jnp.stack(tap_terms).reshape(3, 3, padded.shape[2], flat_back.shape[1])


def forward_conv(padded, conv_weight, extent):
    conv_out = conv_rows(padded, conv_weight, 0, extent, extent)
    return conv_out


def backward_conv(padded, back_grad, conv_weight, extent):
    padded_back = jnp.pad(back_grad, ((1, 1), (1, 1), (0, 0)))
    weight_part = weight_grad_rows(padded, back_grad, 0, extent, extent)
    input_part = input_grad_rows(padded_back, conv_weight, 0, extent, extent)
    return (weight_part, input_part)


def combine_stats(values):
    within = lax.psum(values, "group")
    result = lax.psum(within, "wide")
    return result


def combine_grads(values):
    within = lax.psum(values, "group")
    result = lax.psum(within, "wide")
    return result


def shards(
    feat4,
    feat5,
    feat6,
    feat7,
    out_grad4,
    out_grad5,
    out_grad6,
    out_grad7,
    conv_weight,
    bn_gain,
    bn_shift,
    heights,
    widths,
):
    features = (feat4, feat5, feat6, feat7)
    cotangents = (out_grad4, out_grad5, out_grad6, out_grad7)
    devices = lax.axis_size("wide") * lax.axis_size("group")
    levels = []
    for level_index in range(4):
        feature = features[level_index][0]
        extent = feature.shape[0]
        valid_mask, row_limit = level_mask(heights, widths, 16 * 2**level_index, extent)
        weighted = valid_mask[:, :, None]
        padded = jnp.pad(feature * weighted.astype(feature.dtype), ((1, 1), (1, 1), (0, 0)))
        conv_out = forward_conv(padded, conv_weight, extent)
        levels.append((valid_mask, row_limit, weighted, padded, conv_out))
    moments = []
    local_sums = jnp.stack(
        [jnp.sum(level_entry[4] * level_entry[2], axis=(0, 1)) for level_entry in levels]
    )
    local_squares = jnp.stack(
        [
            jnp.sum(level_entry[2] * level_entry[4] * level_entry[4], axis=(0, 1))
            for level_entry in levels
        ]
    )
    local_counts = jnp.stack([jnp.sum(level_entry[0]) for level_entry in levels])
    moment_sums, squares, counts = combine_stats((local_sums, local_squares, local_counts))
    for level_index in range(4):
        pixel_count = counts[level_index]
        mean_value = moment_sums[level_index] / pixel_count
        moments.append(
            (pixel_count, mean_value, squares[level_index] / pixel_count - mean_value * mean_value)
        )
    finals = []
    for level_index in range(4):
        valid_mask, row_limit, weighted, padded, conv_out = levels[level_index]
        pixel_count, mean_value, variance = moments[level_index]
        inverse = lax.rsqrt(variance + EPSILON)
        normed = (conv_out - mean_value) * inverse
        shifted = bn_gain[level_index] * normed + bn_shift[level_index]
        sigmoid_value = jax.nn.sigmoid(shifted)
        output = (weighted * shifted * sigmoid_value).astype(jnp.bfloat16)
        slope_term = (
            weighted
            * cotangents[level_index][0].astype(jnp.float32)
            * sigmoid_value
            * (1.0 + shifted * (1.0 - sigmoid_value))
        )
        finals.append((output, normed, inverse, slope_term))
    shift_local = jnp.stack([jnp.sum(final_entry[3], axis=(0, 1)) for final_entry in finals])
    gain_local = jnp.stack(
        [jnp.sum(final_entry[3] * final_entry[1], axis=(0, 1)) for final_entry in finals]
    )
    shift_rows, gain_rows = combine_stats((shift_local, gain_local))
    back_sums = [(shift_rows[level_index], gain_rows[level_index]) for level_index in range(4)]
    weight_local = jnp.zeros(conv_weight.shape, jnp.float32)
    outputs = []
    input_grads = []
    shift_list = []
    gain_list = []
    for level_index in range(4):
        valid_mask, row_limit, weighted, padded, conv_out = levels[level_index]
        pixel_count, mean_value, variance = moments[level_index]
        output, normed, inverse, slope_term = finals[level_index]
        shift_sum, gain_sum = back_sums[level_index]
        extent = conv_out.shape[0]
        back_grad = (
            weighted
            * (bn_gain[level_index] * inverse)
            * (slope_term - shift_sum / pixel_count - normed * (gain_sum / pixel_count))
        ).astype(jnp.bfloat16)
        weight_part, input_part = backward_conv(padded, back_grad, conv_weight, extent)
        weight_local = weight_local + weight_part
        input_grads.append((weighted * input_part).astype(jnp.bfloat16)[None])
        outputs.append(output[None])
        shift_list.append(shift_sum)
        gain_list.append(gain_sum)
    weight_total = combine_grads(weight_local)
    return (
        outputs[0],
        outputs[1],
        outputs[2],
        outputs[3],
        input_grads[0],
        input_grads[1],
        input_grads[2],
        input_grads[3],
        weight_total / devices,
        jnp.stack(gain_list) / devices,
        jnp.stack(shift_list) / devices,
    )


def solution(mesh):
    placed = (
        P(("wide", "group"), None, None, None),
        P(("wide", "group"), None, None, None),
        P(("wide", "group"), None, None, None),
        P(("wide", "group"), None, None, None),
        P(("wide", "group"), None, None, None),
        P(("wide", "group"), None, None, None),
        P(("wide", "group"), None, None, None),
        P(("wide", "group"), None, None, None),
        P(),
        P(),
        P(),
        P(("wide", "group")),
        P(("wide", "group")),
    )
    return jax.shard_map(
        shards,
        mesh=mesh,
        in_specs=placed,
        out_specs=(
            P(("wide", "group"), None, None, None),
            P(("wide", "group"), None, None, None),
            P(("wide", "group"), None, None, None),
            P(("wide", "group"), None, None, None),
            P(("wide", "group"), None, None, None),
            P(("wide", "group"), None, None, None),
            P(("wide", "group"), None, None, None),
            P(("wide", "group"), None, None, None),
            P(),
            P(),
            P(),
        ),
        check_vma=False,
    )
```

profile of v0, /device:TPU:0, one launch (start us, length us, event | category | flops | bytes accessed | tf_op | source)
XLA Modules:
  0.0 299.1 jit_solution(16657673691624110499)
XLA Ops:
  8.7 0.7 fusion.283
  9.4 0.7 and_convert_fusion.9
  10.1 0.7 fusion.281
  10.8 0.7 and_convert_fusion.3
  11.5 0.8 bitcast_multiply_fusion.8
  12.2 0.8 broadcast_multiply_fusion.4
  13.0 0.6 fusion.268
  13.8 0.7 fusion.257
  14.5 0.7 and_convert_fusion
  15.2 0.8 bitcast_multiply_fusion.6
  16.0 0.8 broadcast_multiply_fusion.3
  17.4 1.0 fusion.131
  18.4 1.1 convolution_add_fusion.63
  19.4 1.1 convolution_add_fusion.62
  21.9 0.7 multiply_reduce_fusion.6
  22.6 0.6 reshape.1117
  26.4 0.7 multiply_reduce_fusion.4
  27.2 0.6 reshape.1116
  31.1 0.7 reshape.1115
  35.5 2.6 pad_maximum_fusion.4
  38.2 8.7 %all-reduce.11 = (f32[4,256]{1,0:T(4,128)S(1)}, f32[4]{0:T(128)S(1)}, f32[4,256]{1,0:T(4,128)S(1)}) all-reduce(f32[4,256]{1,0:T(4,128)S(1)} %pad_maximum_fusion.1, f32[4]{0:T(128)S(1)} %pad_maximum_fusion.4, f32[4,256]{1,0:T(4,128)S(1)} %pad_maximum_fusion), channel_id=1, replica_groups=mesh['wide'=8,'group'=4] {'group'}, use_global_device_ids=true, to_apply=%region_16.17 | all-reduce | flops 2052 | bytes 16416 | tf_op jit(solution)/shard_map/psum | solution.py:81
  46.9 22.2 %all-reduce.9 = (f32[4,256]{1,0:T(4,128)S(1)}, f32[4]{0:T(128)S(1)}, f32[4,256]{1,0:T(4,128)S(1)}) all-reduce(f32[4,256]{1,0:T(4,128)S(1)} %get-tuple-element.34, f32[4]{0:T(128)S(1)} %get-tuple-element.35, f32[4,256]{1,0:T(4,128)S(1)} %get-tuple-element.36), channel_id=1, replica_groups=mesh['wide'=8,'group'=4] {'wide'}, use_global_device_ids=true, to_apply=%region_17.18 | all-reduce | flops 2052 | bytes 16416 | tf_op jit(solution)/shard_map/psum | solution.py:82
  69.7 2.6 slice_divide_fusion.8
  72.3 2.6 slice_divide_fusion.9
  78.2 0.7 fusion.299
  78.9 5.9 %all-reduce.10 = (f32[4,256]{1,0:T(4,128)S(1)}, f32[4,256]{1,0:T(4,128)S(1)}) all-reduce(f32[4,256]{1,0:T(4,128)S(1)} %pad_maximum_fusion.3, f32[4,256]{1,0:T(4,128)S(1)} %pad_maximum_fusion.2), channel_id=1, replica_groups=mesh['wide'=8,'group'=4] {'group'}, use_global_device_ids=true, to_apply=%region_28.29 | all-reduce | flops 2048 | bytes 16384 | tf_op jit(solution)/shard_map/psum | solution.py:81
  84.8 17.6 %all-reduce.8 = (f32[4,256]{1,0:T(4,128)S(1)}, f32[4,256]{1,0:T(4,128)S(1)}) all-reduce(f32[4,256]{1,0:T(4,128)S(1)} %get-tuple-element.32, f32[4,256]{1,0:T(4,128)S(1)} %get-tuple-element.33), channel_id=1, replica_groups=mesh['wide'=8,'group'=4] {'wide'}, use_global_device_ids=true, to_apply=%region_29.30 | all-reduce | flops 2048 | bytes 16384 | tf_op jit(solution)/shard_map/psum | solution.py:82
  102.4 2.6 slice_divide_fusion
  105.1 2.6 slice_divide_fusion.1
  107.9 1.1 multiply_convert_fusion.2
  110.7 0.6 fusion.4
  120.9 2.1 add_add_fusion
  123.7 0.6 reshape.1164
  124.3 0.7 reshape.1163
  125.6 0.6 pad_slice_fusion.32
  126.2 0.6 pad_slice_fusion.48
  127.0 1.3 reshape.1156
  128.3 1.3 reshape.1150
  129.6 1.3 reshape.1151
  130.9 1.3 reshape.1152
  132.2 1.3 reshape.1153
  133.5 0.7 reshape.1154
  135.0 0.9 convolution_add_fusion.55
  135.9 0.9 convolution_add_fusion.54
  136.8 0.9 convolution_add_fusion.53
  137.6 1.0 convolution_add_fusion.52
  138.6 0.9 convolution_add_fusion.51
  140.1 1.4 multiply_convert_fusion.21
  141.5 0.6 reshape.1141
  142.1 0.6 reshape.1142
  142.7 0.6 reshape.1143
  145.3 0.9 convolution_add_fusion.39
  146.2 0.9 convolution_add_fusion.38
  147.1 0.9 convolution_add_fusion.37
  148.1 1.0 convolution_add_fusion.36
  152.4 0.7 reshape.1139
  153.2 1.2 pad_slice_fusion
  154.4 0.7 multiply_convert_fusion.13
  156.1 20.6 %all-reduce.15.cloned.1.call-done = f32[3,3,256,256]{3,2,1,0:T(8,128)} async-done(((f32[3,3,256,256]{3,2,1,0:T(8,128)}), f32[3,3,256,256]{3,2,1,0:T(8,128)}) %all-reduce.15.cloned.1.call-update) | async-done | bytes 2359312 | tf_op jit(solution)/shard_map/psum | solution.py:87
  176.7 1.9 multiply_convert_fusion.6
  179.4 0.7 copy-done.4
  181.7 1.1 multiply_convert_fusion.1
  182.7 106.2 %all-reduce.17.cloned.1.call-done = f32[3,3,256,256]{3,2,1,0:T(8,128)} async-done(((f32[3,3,256,256]{3,2,1,0:T(8,128)}), f32[3,3,256,256]{3,2,1,0:T(8,128)}) %all-reduce.17.cloned.1.call-update) | async-done | bytes 2359312 | tf_op jit(solution)/shard_map/psum | solution.py:88
  289.0 3.3 %broadcast_multiply_fusion = f32[3,3,256,256]{3,2,1,0:T(8,128)} fusion(f32[3,3,256,256]{3,2,1,0:T(8,128)} %all-reduce.17.cloned.1.call-done), kind=kLoop, calls=%fused_computation.17 | loop fusion | flops 589824 | bytes 4718592 | tf_op jit(solution)/shard_map/div | solution.py:191
  (460 shorter events, 37.0 us)
Async XLA Ops:
  7.2 13.3 %copy-start = (bf16[3,3,256,256]{3,2,1,0:T(8,128)(2,1)S(1)}, bf16[3,3,256,256]{3,2,1,0:T(8,128)(2,1)}, u32[]{:S(2)}) copy-start(bf16[3,3,256,256]{3,2,1,0:T(8,128)(2,1)} %param.21) | copy-start | bytes 3538948
  7.2 16.6 %copy-start.9 = (bf16[1,12,12,256]{3,2,1,0:T(8,128)(2,1)S(1)}, bf16[1,12,12,256]{3,2,1,0:T(8,128)(2,1)}, u32[]{:S(2)}) copy-start(bf16[1,12,12,256]{3,2,1,0:T(8,128)(2,1)} %param.14) | copy-start | bytes 221188
  7.2 169.5 %all-reduce.15.cloned.1.call-start = ((), (), s32[]{:S(2)}) async-start(), calls=%async_computation | async-start | bytes 4718592 | tf_op jit(solution)/shard_map/psum | solution.py:87
  13.0 4.1 %copy-start.76 = (bf16[1,3,3,256]{3,2,1,0:T(4,128)(2,1)}, bf16[1,3,3,256]{3,2,1,0:T(4,128)(2,1)S(1)}, u32[]{:S(2)}) copy-start(bf16[1,3,3,256]{3,2,1,0:T(4,128)(2,1)S(1)} %broadcast_multiply_fusion.4) | copy-start | bytes 13828
  16.0 8.5 %copy-start.28 = (bf16[6,6,256]{2,1,0:T(8,128)(2,1)}, bf16[6,6,256]{2,1,0:T(8,128)(2,1)S(1)}, u32[]{:S(2)}) copy-start(bf16[6,6,256]{2,1,0:T(8,128)(2,1)S(1)} %bitcast_multiply_fusion.6) | copy-start | bytes 55300
  16.8 7.6 %copy-start.33 = (bf16[1,6,6,256]{3,2,1,0:T(8,128)(2,1)}, bf16[1,6,6,256]{3,2,1,0:T(8,128)(2,1)S(1)}, u32[]{:S(2)}) copy-start(bf16[1,6,6,256]{3,2,1,0:T(8,128)(2,1)S(1)} %broadcast_multiply_fusion.3) | copy-start | bytes 55300
  24.0 4.5 %copy-start.12 = (bf16[1,12,12,256]{3,2,1,0:T(8,128)(2,1)}, bf16[1,12,12,256]{3,2,1,0:T(8,128)(2,1)S(1)}, u32[]{:S(2)}) copy-start(bf16[1,12,12,256]{3,2,1,0:T(8,128)(2,1)S(1)} %broadcast_multiply_fusion.2) | copy-start | bytes 221188
  24.6 3.2 %copy-start.2 = (bf16[1,24,24,256]{3,2,1,0:T(8,128)(2,1)S(1)}, bf16[1,24,24,256]{3,2,1,0:T(8,128)(2,1)}, u32[]{:S(2)}) copy-start(bf16[1,24,24,256]{3,2,1,0:T(8,128)(2,1)} %param.13) | copy-start | bytes 884740
  29.9 2.3 copy-start.124
  29.9 2.3 copy-start.125
  32.2 45.2 %copy-start.45 = (f32[1,256]{1,0:T(1,128)}, f32[1,256]{1,0:T(1,128)S(1)}, u32[]{:S(2)}) copy-start(f32[1,256]{1,0:T(1,128)S(1)} %get-tuple-element.118) | copy-start | bytes 3076
  32.2 45.6 %copy-start.66 = (f32[1,256]{1,0:T(1,128)}, f32[1,256]{1,0:T(1,128)S(1)}, u32[]{:S(2)}) copy-start(f32[1,256]{1,0:T(1,128)S(1)} %get-tuple-element.117) | copy-start | bytes 3076
  32.2 45.7 %copy-start.69 = (f32[1,256]{1,0:T(1,128)}, f32[1,256]{1,0:T(1,128)S(1)}, u32[]{:S(2)}) copy-start(f32[1,256]{1,0:T(1,128)S(1)} %get-tuple-element.119) | copy-start | bytes 3076
  32.2 45.9 %copy-start.98 = (f32[1,256]{1,0:T(1,128)}, f32[1,256]{1,0:T(1,128)S(1)}, u32[]{:S(2)}) copy-start(f32[1,256]{1,0:T(1,128)S(1)} %get-tuple-element.116) | copy-start | bytes 3076
  32.3 45.1 %copy-start.56 = (f32[1,256]{1,0:T(1,128)}, f32[1,256]{1,0:T(1,128)S(1)}, u32[]{:S(2)}) copy-start(f32[1,256]{1,0:T(1,128)S(1)} %get-tuple-element.130) | copy-start | bytes 3076
  32.3 45.5 %copy-start.84 = (f32[1,256]{1,0:T(1,128)}, f32[1,256]{1,0:T(1,128)S(1)}, u32[]{:S(2)}) copy-start(f32[1,256]{1,0:T(1,128)S(1)} %get-tuple-element.129) | copy-start | bytes 3076
  32.3 45.7 %copy-start.87 = (f32[1,256]{1,0:T(1,128)}, f32[1,256]{1,0:T(1,128)S(1)}, u32[]{:S(2)}) copy-start(f32[1,256]{1,0:T(1,128)S(1)} %get-tuple-element.131) | copy-start | bytes 3076
  32.3 45.8 %copy-start.100 = (f32[1,256]{1,0:T(1,128)}, f32[1,256]{1,0:T(1,128)S(1)}, u32[]{:S(2)}) copy-start(f32[1,256]{1,0:T(1,128)S(1)} %get-tuple-element.128) | copy-start | bytes 3076
  34.5 3.6 %copy-start.118 = (f32[256]{0:T(256)S(1)}, f32[256]{0:T(256)}, u32[]{:S(2)}) copy-start(f32[256]{0:T(256)} %get-tuple-element.23) | copy-start | bytes 3076
  34.5 3.6 %copy-start.120 = (f32[256]{0:T(256)S(1)}, f32[256]{0:T(256)}, u32[]{:S(2)}) copy-start(f32[256]{0:T(256)} %get-tuple-element.21) | copy-start | bytes 3076
  34.5 3.6 %copy-start.117 = (f32[256]{0:T(256)S(1)}, f32[256]{0:T(256)}, u32[]{:S(2)}) copy-start(f32[256]{0:T(256)} %get-tuple-element.24) | copy-start | bytes 3076
  34.5 3.6 %copy-start.119 = (f32[256]{0:T(256)S(1)}, f32[256]{0:T(256)}, u32[]{:S(2)}) copy-start(f32[256]{0:T(256)} %get-tuple-element.22) | copy-start | bytes 3076
  34.6 42.8 %copy-start.1 = (bf16[1,24,24,256]{3,2,1,0:T(8,128)(2,1)S(1)}, bf16[1,24,24,256]{3,2,1,0:T(8,128)(2,1)}, u32[]{:S(2)}) copy-start(bf16[1,24,24,256]{3,2,1,0:T(8,128)(2,1)} %param.17) | copy-start | bytes 884740
  34.6 42.8 %copy-start.18 = (f32[24,24]{1,0:T(8,128)S(1)}, f32[24,24]{1,0:T(8,128)}, u32[]{:S(2)}) copy-start(f32[24,24]{1,0:T(8,128)} %get-tuple-element.150) | copy-start | bytes 6916
  35.2 42.6 %copy-start.7 = (bf16[1,12,12,256]{3,2,1,0:T(8,128)(2,1)S(1)}, bf16[1,12,12,256]{3,2,1,0:T(8,128)(2,1)}, u32[]{:S(2)}) copy-start(bf16[1,12,12,256]{3,2,1,0:T(8,128)(2,1)} %param.18) | copy-start | bytes 221188
  35.2 42.8 %copy-start.16 = (bf16[1,6,6,256]{3,2,1,0:T(8,128)(2,1)S(1)}, bf16[1,6,6,256]{3,2,1,0:T(8,128)(2,1)}, u32[]{:S(2)}) copy-start(bf16[1,6,6,256]{3,2,1,0:T(8,128)(2,1)} %param.19) | copy-start | bytes 55300
  35.2 42.8 %copy-start.37 = (f32[6,6]{1,0:T(8,128)S(1)}, f32[6,6]{1,0:T(8,128)}, u32[]{:S(2)}) copy-start(f32[6,6]{1,0:T(8,128)} %get-tuple-element.146) | copy-start | bytes 436
  35.2 43.0 %copy-start.26 = (f32[3,3,256]{2,1,0:T(4,128)S(1)}, f32[3,3,256]{2,1,0:T(4,128)}, u32[]{:S(2)}) copy-start(f32[3,3,256]{2,1,0:T(4,128)} %reshape.1121) | copy-start | bytes 27652
  35.2 43.0 %copy-start.48 = (f32[3,3]{1,0:T(4,128)S(1)}, f32[3,3]{1,0:T(4,128)}, u32[]{:S(2)}) copy-start(f32[3,3]{1,0:T(4,128)} %get-tuple-element.144) | copy-start | bytes 112
  35.2 43.0 %copy-start.74 = (bf16[1,3,3,256]{3,2,1,0:T(4,128)(2,1)S(1)}, bf16[1,3,3,256]{3,2,1,0:T(4,128)(2,1)}, u32[]{:S(2)}) copy-start(bf16[1,3,3,256]{3,2,1,0:T(4,128)(2,1)} %param.20) | copy-start | bytes 13828
  75.0 32.8 %copy-start.42 = (f32[1,256]{1,0:T(1,128)}, f32[1,256]{1,0:T(1,128)S(1)}, u32[]{:S(2)}) copy-start(f32[1,256]{1,0:T(1,128)S(1)} %get-tuple-element.123) | copy-start | bytes 3076
  75.0 32.8 %copy-start.60 = (f32[1,256]{1,0:T(1,128)}, f32[1,256]{1,0:T(1,128)S(1)}, u32[]{:S(2)}) copy-start(f32[1,256]{1,0:T(1,128)S(1)} %get-tuple-element.122) | copy-start | bytes 3076
  75.0 32.8 %copy-start.63 = (f32[1,256]{1,0:T(1,128)}, f32[1,256]{1,0:T(1,128)S(1)}, u32[]{:S(2)}) copy-start(f32[1,256]{1,0:T(1,128)S(1)} %get-tuple-element.121) | copy-start | bytes 3076
  75.0 32.8 %copy-start.72 = (f32[1,256]{1,0:T(1,128)}, f32[1,256]{1,0:T(1,128)S(1)}, u32[]{:S(2)}) copy-start(f32[1,256]{1,0:T(1,128)S(1)} %get-tuple-element.120) | copy-start | bytes 3076
  75.6 32.2 %copy-start.81 = (f32[256]{0:T(256)}, f32[256]{0:T(256)S(1)}, u32[]{:S(2)}) copy-start(f32[256]{0:T(256)S(1)} %get-tuple-element.137) | copy-start | bytes 3076
  76.2 31.6 %copy-start.92 = (f32[256]{0:T(256)}, f32[256]{0:T(256)S(1)}, u32[]{:S(2)}) copy-start(f32[256]{0:T(256)S(1)} %get-tuple-element.135) | copy-start | bytes 3076
  76.8 31.1 %copy-start.78 = (f32[256]{0:T(256)}, f32[256]{0:T(256)S(1)}, u32[]{:S(2)}) copy-start(f32[256]{0:T(256)S(1)} %get-tuple-element.139) | copy-start | bytes 3076
  77.4 30.5 %copy-start.52 = (f32[256]{0:T(256)}, f32[256]{0:T(256)S(1)}, u32[]{:S(2)}) copy-start(f32[256]{0:T(256)S(1)} %get-tuple-element.141) | copy-start | bytes 3076
  102.4 5.5 %copy-start.94 = (f32[4,256]{1,0:T(4,128)}, f32[4,256]{1,0:T(4,128)S(1)}, u32[]{:S(2)}) copy-start(f32[4,256]{1,0:T(4,128)S(1)} %get-tuple-element.28) | copy-start | bytes 12292
  102.4 5.5 %copy-start.96 = (f32[4,256]{1,0:T(4,128)}, f32[4,256]{1,0:T(4,128)S(1)}, u32[]{:S(2)}) copy-start(f32[4,256]{1,0:T(4,128)S(1)} %get-tuple-element.27) | copy-start | bytes 12292
  105.0 5.3 %copy-start.104 = (f32[1,256]{1,0:T(1,128)}, f32[1,256]{1,0:T(1,128)S(1)}, u32[]{:S(2)}) copy-start(f32[1,256]{1,0:T(1,128)S(1)} %get-tuple-element.113) | copy-start | bytes 3076
  105.0 9.1 %copy-start.115 = (f32[1,256]{1,0:T(1,128)}, f32[1,256]{1,0:T(1,128)S(1)}, u32[]{:S(2)}) copy-start(f32[1,256]{1,0:T(1,128)S(1)} %get-tuple-element.111) | copy-start | bytes 3076
  105.1 11.6 %copy-start.122 = (f32[1,256]{1,0:T(1,128)}, f32[1,256]{1,0:T(1,128)S(1)}, u32[]{:S(2)}) copy-start(f32[1,256]{1,0:T(1,128)S(1)} %get-tuple-element.110) | copy-start | bytes 3076
  105.1 14.1 %copy-start.111 = (f32[1,256]{1,0:T(1,128)}, f32[1,256]{1,0:T(1,128)S(1)}, u32[]{:S(2)}) copy-start(f32[1,256]{1,0:T(1,128)S(1)} %get-tuple-element.112) | copy-start | bytes 3076
  107.7 2.6 copy-start.106
  107.7 6.4 %copy-start.116 = (f32[1,256]{1,0:T(1,128)}, f32[1,256]{1,0:T(1,128)S(1)}, u32[]{:S(2)}) copy-start(f32[1,256]{1,0:T(1,128)S(1)} %get-tuple-element.107) | copy-start | bytes 3076
  107.7 9.0 %copy-start.123 = (f32[1,256]{1,0:T(1,128)}, f32[1,256]{1,0:T(1,128)S(1)}, u32[]{:S(2)}) copy-start(f32[1,256]{1,0:T(1,128)S(1)} %get-tuple-element.106) | copy-start | bytes 3076
  107.7 11.4 %copy-start.113 = (f32[1,256]{1,0:T(1,128)}, f32[1,256]{1,0:T(1,128)S(1)}, u32[]{:S(2)}) copy-start(f32[1,256]{1,0:T(1,128)S(1)} %get-tuple-element.108) | copy-start | bytes 3076
  118.2 2.5 copy-start.10
  123.0 3.9 %copy-start.11 = (bf16[12,12,256]{2,1,0:T(8,128)(2,1)S(1)}, bf16[12,12,256]{2,1,0:T(8,128)(2,1)}, u32[]{:S(2)}) copy-start(bf16[12,12,256]{2,1,0:T(8,128)(2,1)} %copy-done.10) | copy-start | bytes 221188
  123.0 14.6 %copy-start.25 = (f32[9,256]{1,0:T(8,128)S(1)}, f32[9,256]{1,0:T(8,128)}, u32[]{:S(2)}) copy-start(f32[9,256]{1,0:T(8,128)} %copy-done.24) | copy-start | bytes 27652
  123.0 165.9 %all-reduce.17.cloned.1.call-start = ((), (), s32[]{:S(2)}) async-start(), calls=%async_computation.1 | async-start | bytes 4718592 | tf_op jit(solution)/shard_map/psum | solution.py:88
  126.9 14.5 %copy-start.32 = (bf16[6,6,256]{2,1,0:T(8,128)(2,1)S(1)}, bf16[6,6,256]{2,1,0:T(8,128)(2,1)}, u32[]{:S(2)}) copy-start(bf16[6,6,256]{2,1,0:T(8,128)(2,1)} %get-tuple-element.70) | copy-start | bytes 55300
  126.9 14.5 %copy-start.31 = (bf16[6,6,256]{2,1,0:T(8,128)(2,1)S(1)}, bf16[6,6,256]{2,1,0:T(8,128)(2,1)}, u32[]{:S(2)}) copy-start(bf16[6,6,256]{2,1,0:T(8,128)(2,1)} %get-tuple-element.71) | copy-start | bytes 55300
  127.0 15.2 %copy-start.30 = (bf16[6,6,256]{2,1,0:T(8,128)(2,1)S(1)}, bf16[6,6,256]{2,1,0:T(8,128)(2,1)}, u32[]{:S(2)}) copy-start(bf16[6,6,256]{2,1,0:T(8,128)(2,1)} %get-tuple-element.72) | copy-start | bytes 55300
  134.8 4.8 %copy-start.51 = (bf16[9,256]{1,0:T(8,128)(2,1)S(1)}, bf16[9,256]{1,0:T(8,128)(2,1)}, u32[]{:S(2)}) copy-start(bf16[9,256]{1,0:T(8,128)(2,1)} %reshape.1155) | copy-start | bytes 13828
  134.8 5.0 %copy-start.50 = (bf16[9,256]{1,0:T(8,128)(2,1)S(1)}, bf16[9,256]{1,0:T(8,128)(2,1)}, u32[]{:S(2)}) copy-start(bf16[9,256]{1,0:T(8,128)(2,1)} %reshape.1156) | copy-start | bytes 13828
  144.8 3.3 %copy-start.15 = (f32[36,256]{1,0:T(8,128)S(1)}, f32[36,256]{1,0:T(8,128)}, u32[]{:S(2)}) copy-start(f32[36,256]{1,0:T(8,128)} %copy-done.14) | copy-start | bytes 110596
  144.8 3.3 %copy-start.65 = (f32[1,256]{1,0:T(1,128)S(1)}, f32[1,256]{1,0:T(1,128)}, u32[]{:S(2)}) copy-start(f32[1,256]{1,0:T(1,128)} %copy-done.63) | copy-start | bytes 3076
  144.8 3.3 %copy-start.71 = (f32[1,256]{1,0:T(1,128)S(1)}, f32[1,256]{1,0:T(1,128)}, u32[]{:S(2)}) copy-start(f32[1,256]{1,0:T(1,128)} %copy-done.69) | copy-start | bytes 3076
  144.8 3.3 %copy-start.83 = (f32[256]{0:T(256)S(1)}, f32[256]{0:T(256)}, u32[]{:S(2)}) copy-start(f32[256]{0:T(256)} %copy-done.81) | copy-start | bytes 3076
  144.8 3.3 %copy-start.89 = (f32[1,256]{1,0:T(1,128)S(1)}, f32[1,256]{1,0:T(1,128)}, u32[]{:S(2)}) copy-start(f32[1,256]{1,0:T(1,128)} %copy-done.87) | copy-start | bytes 3076
  144.9 4.2 %copy-start.36 = (bf16[36,256]{1,0:T(8,128)(2,1)S(1)}, bf16[36,256]{1,0:T(8,128)(2,1)}, u32[]{:S(2)}) copy-start(bf16[36,256]{1,0:T(8,128)(2,1)} %reshape.1144) | copy-start | bytes 55300
  145.0 4.4 %copy-start.35 = (bf16[36,256]{1,0:T(8,128)(2,1)S(1)}, bf16[36,256]{1,0:T(8,128)(2,1)}, u32[]{:S(2)}) copy-start(bf16[36,256]{1,0:T(8,128)(2,1)} %reshape.1145) | copy-start | bytes 55300
  (65 other events, 87.7 us)
Sparse Core Ops, SparseCore 0:
  123.2 53.5 all-reduce.14
  180.3 108.6 all-reduce.16
where the time goes:
time: 301 us; the launch traced here: 299 us
  waiting for transfers between devices  127 us (42%)
  blocking collectives  54.4 us (18%)
  other arithmetic  41.2 us (14%)
  matrix products  34 us (11%)
  local copies, waits for them, and re-layouts  24.6 us (8%)
  between operations  18.1 us (6%)
    psum x1, waiting for transfers between devices, combine_grads(): result = lax.psum(within, 'wide')  106 us
    psum x2, blocking collectives, combine_stats(): result = lax.psum(within, 'wide')  39.7 us
    psum x1, waiting for transfers between devices, combine_grads(): within = lax.psum(values, 'group')  20.6 us
    psum x2, blocking collectives, combine_stats(): within = lax.psum(values, 'group')  14.6 us
    dot_general x36, matrix products, input_grad_rows(): lax.dot_general(window.reshape(row_count * extent, -1), conv_weight[tap_r...  14.1 us
    reshape x24, local copies, waits for them, and re-layouts, input_grad_rows(): window.reshape(row_count * extent, -1)  11.1 us
    dot_general x36, matrix products, conv_rows(): jnp.dot(window.reshape(row_count * extent, -1), conv_weight[tap_row, tap_...  10.4 us
    dot_general x36, matrix products, weight_grad_rows(): lax.dot_general(window.reshape(row_count * extent, -1), flat_back, (((0,)...  9.51 us
  transfers between devices with their start and end apart: 2, of which 2 were waited for; matrix products, arithmetic and copies ran while one was open for 12% of the time, Pallas kernels for 0%

commit v1 on v0

--- a/solution.py
+++ b/solution.py
@@ -85,7 +85,9 @@
 
 def combine_grads(values):
     within = lax.psum(values, "group")
-    result = lax.psum(within, "wide")
+    result = within
+    for hop in (1, 2, 4):
+        result = result + lax.ppermute(result, "wide", [(dev, dev ^ hop) for dev in range(8)])
     return result
 
 

time: 301 us -> 399 us (1.33)
  waiting for transfers between devices: 127 us -> 234 us
  local copies, waits for them, and re-layouts: 24.6 us -> 14.1 us
  starting transfers between devices: 0.08 us -> 5.46 us
  matrix products: 34 us -> 29.3 us
    ppermute x0 -> x3, waiting for transfers between devices: none -> 184 us  [combine_grads(): lax.ppermute(result, 'wide', [(dev, dev ^ hop) for dev in range(8)])]
    psum x1 -> x0, waiting for transfers between devices: 106 us -> none  [combine_grads(): result = lax.psum(within, 'wide')]
    psum x1, waiting for transfers between devices: 20.6 us -> 49.5 us  [combine_grads(): within = lax.psum(values, 'group')]
    reshape x24, local copies, waits for them, and re-layouts: 11.1 us -> 3.2 us  [input_grad_rows(): window.reshape(row_count * extent, -1)]
    add x0 -> x2, other arithmetic: none -> 6.06 us  [combine_grads(): result + lax.ppermute(result, 'wide', [(dev, dev ^ hop) for dev in range(...]
    ppermute x0 -> x3, starting transfers between devices: none -> 5.42 us  [combine_grads(): lax.ppermute(result, 'wide', [(dev, dev ^ hop) for dev in range(8)])]
    dot_general x36, matrix products: 14.1 us -> 9.39 us  [input_grad_rows(): lax.dot_general(window.reshape(row_count * extent, -1), conv_weight[tap_r...]
  transfers between devices with their start and end apart: 2 -> 4, of which waited for: 2 -> 4; matrix products, arithmetic and copies ran while one was open for 12% -> 5% of each run, Pallas kernels for 0% -> 0%
where the time goes in v1:
time: 399 us; the launch traced here: 398 us
  waiting for transfers between devices  234 us (59%)
  blocking collectives  54.3 us (14%)
  other arithmetic  42.7 us (11%)
  matrix products  29.3 us (7%)
  between operations  18.2 us (5%)
  local copies, waits for them, and re-layouts  14.1 us (4%)
  starting transfers between devices  5.46 us (1%)
    ppermute x3, waiting for transfers between devices, combine_grads(): lax.ppermute(result, 'wide', [(dev, dev ^ hop) for dev in range(8)])  184 us
    psum x1, waiting for transfers between devices, combine_grads(): within = lax.psum(values, 'group')  49.5 us
    psum x2, blocking collectives, combine_stats(): result = lax.psum(within, 'wide')  39.7 us
    psum x2, blocking collectives, combine_stats(): within = lax.psum(values, 'group')  14.6 us
    dot_general x36, matrix products, conv_rows(): jnp.dot(window.reshape(row_count * extent, -1), conv_weight[tap_row, tap_...  10.4 us
    dot_general x36, matrix products, weight_grad_rows(): lax.dot_general(window.reshape(row_count * extent, -1), flat_back, (((0,)...  9.51 us
    dot_general x36, matrix products, input_grad_rows(): lax.dot_general(window.reshape(row_count * extent, -1), conv_weight[tap_r...  9.39 us
  transfers between devices with their start and end apart: 4, of which 4 were waited for; matrix products, arithmetic and copies ran while one was open for 5% of the time, Pallas kernels for 0%

profile of v1, /device:TPU:0, one launch (start us, length us, event | category | flops | bytes accessed | tf_op | source)
XLA Modules:
  0.0 398.0 jit_solution(6705998173099270674)
XLA Ops:
  8.7 0.7 fusion.283
  9.5 0.6 and_convert_fusion.9
  10.1 0.7 fusion.281
  10.8 0.7 and_convert_fusion.3
  11.5 0.8 bitcast_multiply_fusion.8
  12.2 0.8 broadcast_multiply_fusion.3
  13.0 0.7 fusion.268
  13.8 0.7 fusion.257
  14.5 0.7 and_convert_fusion
  15.2 0.8 bitcast_multiply_fusion.6
  16.0 0.8 broadcast_multiply_fusion.2
  17.4 1.0 fusion.131
  18.4 1.1 convolution_add_fusion.63
  19.5 1.1 convolution_add_fusion.62
  21.9 0.7 multiply_reduce_fusion.6
  22.6 0.6 reshape.1117
  23.2 0.6 reshape.1121
  25.9 0.6 and_convert_fusion.6
  26.5 0.7 multiply_reduce_fusion.4
  27.2 0.6 reshape.1116
  31.1 0.7 reshape.1115
  34.6 0.6 and_convert_fusion.2
  35.5 2.6 pad_maximum_fusion.4
  38.2 8.7 %all-reduce.11 = (f32[4,256]{1,0:T(4,128)S(1)}, f32[4]{0:T(128)S(1)}, f32[4,256]{1,0:T(4,128)S(1)}) all-reduce(f32[4,256]{1,0:T(4,128)S(1)} %pad_maximum_fusion.1, f32[4]{0:T(128)S(1)} %pad_maximum_fusion.4, f32[4,256]{1,0:T(4,128)S(1)} %pad_maximum_fusion), channel_id=1, replica_groups=mesh['wide'=8,'group'=4] {'group'}, use_global_device_ids=true, to_apply=%region_16.17 | all-reduce | flops 2052 | bytes 16416 | tf_op jit(solution)/shard_map/psum | solution.py:81
  46.9 22.2 %all-reduce.9 = (f32[4,256]{1,0:T(4,128)S(1)}, f32[4]{0:T(128)S(1)}, f32[4,256]{1,0:T(4,128)S(1)}) all-reduce(f32[4,256]{1,0:T(4,128)S(1)} %get-tuple-element.34, f32[4]{0:T(128)S(1)} %get-tuple-element.35, f32[4,256]{1,0:T(4,128)S(1)} %get-tuple-element.36), channel_id=1, replica_groups=mesh['wide'=8,'group'=4] {'wide'}, use_global_device_ids=true, to_apply=%region_17.18 | all-reduce | flops 2052 | bytes 16416 | tf_op jit(solution)/shard_map/psum | solution.py:82
  69.1 0.7 fusion.303
  69.7 2.4 slice_divide_fusion.8
  72.1 2.4 slice_divide_fusion.9
  74.5 0.6 fusion.286
  75.1 0.6 fusion.285
  77.6 0.7 fusion.299
  78.3 5.9 %all-reduce.10 = (f32[4,256]{1,0:T(4,128)S(1)}, f32[4,256]{1,0:T(4,128)S(1)}) all-reduce(f32[4,256]{1,0:T(4,128)S(1)} %pad_maximum_fusion.3, f32[4,256]{1,0:T(4,128)S(1)} %pad_maximum_fusion.2), channel_id=1, replica_groups=mesh['wide'=8,'group'=4] {'group'}, use_global_device_ids=true, to_apply=%region_28.29 | all-reduce | flops 2048 | bytes 16384 | tf_op jit(solution)/shard_map/psum | solution.py:81
  84.2 17.6 %all-reduce.8 = (f32[4,256]{1,0:T(4,128)S(1)}, f32[4,256]{1,0:T(4,128)S(1)}) all-reduce(f32[4,256]{1,0:T(4,128)S(1)} %get-tuple-element.32, f32[4,256]{1,0:T(4,128)S(1)} %get-tuple-element.33), channel_id=1, replica_groups=mesh['wide'=8,'group'=4] {'wide'}, use_global_device_ids=true, to_apply=%region_29.30 | all-reduce | flops 2048 | bytes 16384 | tf_op jit(solution)/shard_map/psum | solution.py:82
  101.8 2.4 slice_divide_fusion
  104.2 2.4 slice_divide_fusion.1
  106.7 1.1 multiply_convert_fusion.2
  109.5 0.6 fusion.4
  119.8 2.1 add_add_fusion
  121.9 0.6 pad_slice_fusion.32
  124.2 0.8 convolution_add_fusion.49
  126.1 49.5 %all-reduce.14.cloned.1.call-done = f32[3,3,256,256]{3,2,1,0:T(8,128)} async-done(((f32[3,3,256,256]{3,2,1,0:T(8,128)}), f32[3,3,256,256]{3,2,1,0:T(8,128)}) %all-reduce.14.cloned.1.call-update) | async-done | bytes 2359312 | tf_op jit(solution)/shard_map/psum | solution.py:87
  175.6 1.5 collective-permute-start
  177.0 0.7 pad_slice_fusion.16
  177.8 0.7 reshape.1163
  178.5 0.6 reshape.1146
  179.1 1.5 reshape.1132
  180.7 0.7 reshape.1133
  181.7 0.9 convolution_add_fusion.33
  182.6 0.8 convolution_add_fusion.32
  185.1 43.6 %collective-permute-done = f32[3,3,256,256]{3,2,1,0:T(8,128)} collective-permute-done((f32[3,3,256,256]{3,2,1,0:T(8,128)}, f32[3,3,256,256]{3,2,1,0:T(8,128)}, u32[]{:S(2)}, u32[]{:S(2)}) %collective-permute-start) | collective-permute-done | bytes 2359328 | tf_op jit(solution)/shard_map/ppermute | solution.py:90
  228.6 3.4 add.721
  232.0 1.5 collective-permute-start.1
  233.7 0.6 reshape.1157
  235.6 0.6 broadcast_multiply_fusion.5
  236.2 0.6 broadcast_multiply_fusion.4
  236.8 0.7 multiply_convert_fusion.21
  237.5 0.7 multiply_convert_fusion.13
  239.3 44.9 %collective-permute-done.1 = f32[3,3,256,256]{3,2,1,0:T(8,128)} collective-permute-done((f32[3,3,256,256]{3,2,1,0:T(8,128)}, f32[3,3,256,256]{3,2,1,0:T(8,128)}, u32[]{:S(2)}, u32[]{:S(2)}) %collective-permute-start.1) | collective-permute-done | bytes 2359328 | tf_op jit(solution)/shard_map/ppermute | solution.py:90
  284.2 2.7 add.722
  286.9 2.5 collective-permute-start.2
  289.4 0.8 multiply_convert_fusion.6
  292.5 1.1 multiply_convert_fusion.1
  293.6 95.9 %collective-permute-done.2 = f32[3,3,256,256]{3,2,1,0:T(8,128)S(1)} collective-permute-done((f32[3,3,256,256]{3,2,1,0:T(8,128)S(1)}, f32[3,3,256,256]{3,2,1,0:T(8,128)S(1)}, u32[]{:S(2)}, u32[]{:S(2)}) %collective-permute-start.2) | collective-permute-done | bytes 2359328 | tf_op jit(solution)/shard_map/ppermute | solution.py:90
  389.4 1.7 add_multiply_fusion
  (481 shorter events, 31.3 us)
Async XLA Ops:
  7.2 13.4 %copy-start = (bf16[3,3,256,256]{3,2,1,0:T(8,128)(2,1)S(1)}, bf16[3,3,256,256]{3,2,1,0:T(8,128)(2,1)}, u32[]{:S(2)}) copy-start(bf16[3,3,256,256]{3,2,1,0:T(8,128)(2,1)} %param.21) | copy-start | bytes 3538948
  7.2 16.6 %copy-start.7 = (bf16[1,12,12,256]{3,2,1,0:T(8,128)(2,1)S(1)}, bf16[1,12,12,256]{3,2,1,0:T(8,128)(2,1)}, u32[]{:S(2)}) copy-start(bf16[1,12,12,256]{3,2,1,0:T(8,128)(2,1)} %param.14) | copy-start | bytes 221188
  7.2 168.4 %all-reduce.14.cloned.1.call-start = ((), (), s32[]{:S(2)}) async-start(), calls=%async_computation | async-start | bytes 4718592 | tf_op jit(solution)/shard_map/psum | solution.py:87
  13.0 4.2 %copy-start.74 = (bf16[1,3,3,256]{3,2,1,0:T(4,128)(2,1)}, bf16[1,3,3,256]{3,2,1,0:T(4,128)(2,1)S(1)}, u32[]{:S(2)}) copy-start(bf16[1,3,3,256]{3,2,1,0:T(4,128)(2,1)S(1)} %broadcast_multiply_fusion.3) | copy-start | bytes 13828
  16.0 8.4 %copy-start.27 = (bf16[6,6,256]{2,1,0:T(8,128)(2,1)}, bf16[6,6,256]{2,1,0:T(8,128)(2,1)S(1)}, u32[]{:S(2)}) copy-start(bf16[6,6,256]{2,1,0:T(8,128)(2,1)S(1)} %bitcast_multiply_fusion.6) | copy-start | bytes 55300
  16.8 7.5 %copy-start.29 = (bf16[1,6,6,256]{3,2,1,0:T(8,128)(2,1)}, bf16[1,6,6,256]{3,2,1,0:T(8,128)(2,1)S(1)}, u32[]{:S(2)}) copy-start(bf16[1,6,6,256]{3,2,1,0:T(8,128)(2,1)S(1)} %broadcast_multiply_fusion.2) | copy-start | bytes 55300
  24.0 4.5 %copy-start.8 = (bf16[1,12,12,256]{3,2,1,0:T(8,128)(2,1)}, bf16[1,12,12,256]{3,2,1,0:T(8,128)(2,1)S(1)}, u32[]{:S(2)}) copy-start(bf16[1,12,12,256]{3,2,1,0:T(8,128)(2,1)S(1)} %broadcast_multiply_fusion.1) | copy-start | bytes 221188
  24.6 3.3 copy-start.3
  32.2 44.6 %copy-start.42 = (f32[1,256]{1,0:T(1,128)}, f32[1,256]{1,0:T(1,128)S(1)}, u32[]{:S(2)}) copy-start(f32[1,256]{1,0:T(1,128)S(1)} %get-tuple-element.118) | copy-start | bytes 3076
  32.2 45.0 %copy-start.61 = (f32[1,256]{1,0:T(1,128)}, f32[1,256]{1,0:T(1,128)S(1)}, u32[]{:S(2)}) copy-start(f32[1,256]{1,0:T(1,128)S(1)} %get-tuple-element.117) | copy-start | bytes 3076
  32.2 45.2 %copy-start.65 = (f32[1,256]{1,0:T(1,128)}, f32[1,256]{1,0:T(1,128)S(1)}, u32[]{:S(2)}) copy-start(f32[1,256]{1,0:T(1,128)S(1)} %get-tuple-element.119) | copy-start | bytes 3076
  32.2 45.3 %copy-start.98 = (f32[1,256]{1,0:T(1,128)}, f32[1,256]{1,0:T(1,128)S(1)}, u32[]{:S(2)}) copy-start(f32[1,256]{1,0:T(1,128)S(1)} %get-tuple-element.116) | copy-start | bytes 3076
  32.3 44.6 %copy-start.51 = (f32[1,256]{1,0:T(1,128)}, f32[1,256]{1,0:T(1,128)S(1)}, u32[]{:S(2)}) copy-start(f32[1,256]{1,0:T(1,128)S(1)} %get-tuple-element.130) | copy-start | bytes 3076
  32.3 45.0 %copy-start.83 = (f32[1,256]{1,0:T(1,128)}, f32[1,256]{1,0:T(1,128)S(1)}, u32[]{:S(2)}) copy-start(f32[1,256]{1,0:T(1,128)S(1)} %get-tuple-element.129) | copy-start | bytes 3076
  32.3 45.1 %copy-start.87 = (f32[1,256]{1,0:T(1,128)}, f32[1,256]{1,0:T(1,128)S(1)}, u32[]{:S(2)}) copy-start(f32[1,256]{1,0:T(1,128)S(1)} %get-tuple-element.131) | copy-start | bytes 3076
  32.3 45.3 %copy-start.101 = (f32[1,256]{1,0:T(1,128)}, f32[1,256]{1,0:T(1,128)S(1)}, u32[]{:S(2)}) copy-start(f32[1,256]{1,0:T(1,128)S(1)} %get-tuple-element.128) | copy-start | bytes 3076
  34.5 3.6 copy-start.122
  34.5 3.6 copy-start.124
  34.5 3.6 copy-start.121
  34.6 3.6 copy-start.123
  34.6 42.3 %copy-start.1 = (bf16[1,24,24,256]{3,2,1,0:T(8,128)(2,1)S(1)}, bf16[1,24,24,256]{3,2,1,0:T(8,128)(2,1)}, u32[]{:S(2)}) copy-start(bf16[1,24,24,256]{3,2,1,0:T(8,128)(2,1)} %param.17) | copy-start | bytes 884740
  34.6 42.3 %copy-start.16 = (f32[24,24]{1,0:T(8,128)S(1)}, f32[24,24]{1,0:T(8,128)}, u32[]{:S(2)}) copy-start(f32[24,24]{1,0:T(8,128)} %get-tuple-element.150) | copy-start | bytes 6916
  35.2 42.1 %copy-start.4 = (bf16[1,12,12,256]{3,2,1,0:T(8,128)(2,1)S(1)}, bf16[1,12,12,256]{3,2,1,0:T(8,128)(2,1)}, u32[]{:S(2)}) copy-start(bf16[1,12,12,256]{3,2,1,0:T(8,128)(2,1)} %param.18) | copy-start | bytes 221188
  35.2 42.3 %copy-start.14 = (bf16[1,6,6,256]{3,2,1,0:T(8,128)(2,1)S(1)}, bf16[1,6,6,256]{3,2,1,0:T(8,128)(2,1)}, u32[]{:S(2)}) copy-start(bf16[1,6,6,256]{3,2,1,0:T(8,128)(2,1)} %param.19) | copy-start | bytes 55300
  35.2 42.3 %copy-start.32 = (f32[6,6]{1,0:T(8,128)S(1)}, f32[6,6]{1,0:T(8,128)}, u32[]{:S(2)}) copy-start(f32[6,6]{1,0:T(8,128)} %get-tuple-element.146) | copy-start | bytes 436
  35.2 42.4 %copy-start.25 = (f32[3,3,256]{2,1,0:T(4,128)S(1)}, f32[3,3,256]{2,1,0:T(4,128)}, u32[]{:S(2)}) copy-start(f32[3,3,256]{2,1,0:T(4,128)} %reshape.1121) | copy-start | bytes 27652
  35.2 42.4 %copy-start.45 = (f32[3,3]{1,0:T(4,128)S(1)}, f32[3,3]{1,0:T(4,128)}, u32[]{:S(2)}) copy-start(f32[3,3]{1,0:T(4,128)} %get-tuple-element.144) | copy-start | bytes 112
  35.2 42.4 %copy-start.72 = (bf16[1,3,3,256]{3,2,1,0:T(4,128)(2,1)S(1)}, bf16[1,3,3,256]{3,2,1,0:T(4,128)(2,1)}, u32[]{:S(2)}) copy-start(bf16[1,3,3,256]{3,2,1,0:T(4,128)(2,1)} %param.20) | copy-start | bytes 13828
  74.5 32.1 %copy-start.39 = (f32[1,256]{1,0:T(1,128)}, f32[1,256]{1,0:T(1,128)S(1)}, u32[]{:S(2)}) copy-start(f32[1,256]{1,0:T(1,128)S(1)} %get-tuple-element.123) | copy-start | bytes 3076
  74.5 32.1 %copy-start.54 = (f32[1,256]{1,0:T(1,128)}, f32[1,256]{1,0:T(1,128)S(1)}, u32[]{:S(2)}) copy-start(f32[1,256]{1,0:T(1,128)S(1)} %get-tuple-element.122) | copy-start | bytes 3076
  74.5 32.1 %copy-start.58 = (f32[1,256]{1,0:T(1,128)}, f32[1,256]{1,0:T(1,128)S(1)}, u32[]{:S(2)}) copy-start(f32[1,256]{1,0:T(1,128)S(1)} %get-tuple-element.121) | copy-start | bytes 3076
  74.5 32.1 %copy-start.68 = (f32[1,256]{1,0:T(1,128)}, f32[1,256]{1,0:T(1,128)S(1)}, u32[]{:S(2)}) copy-start(f32[1,256]{1,0:T(1,128)S(1)} %get-tuple-element.120) | copy-start | bytes 3076
  75.1 31.5 %copy-start.80 = (f32[256]{0:T(256)}, f32[256]{0:T(256)S(1)}, u32[]{:S(2)}) copy-start(f32[256]{0:T(256)S(1)} %get-tuple-element.137) | copy-start | bytes 3076
  75.7 31.0 %copy-start.91 = (f32[256]{0:T(256)}, f32[256]{0:T(256)S(1)}, u32[]{:S(2)}) copy-start(f32[256]{0:T(256)S(1)} %get-tuple-element.135) | copy-start | bytes 3076
  76.3 30.4 %copy-start.76 = (f32[256]{0:T(256)}, f32[256]{0:T(256)S(1)}, u32[]{:S(2)}) copy-start(f32[256]{0:T(256)S(1)} %get-tuple-element.139) | copy-start | bytes 3076
  76.8 29.9 %copy-start.48 = (f32[256]{0:T(256)}, f32[256]{0:T(256)S(1)}, u32[]{:S(2)}) copy-start(f32[256]{0:T(256)S(1)} %get-tuple-element.141) | copy-start | bytes 3076
  101.8 4.9 %copy-start.94 = (f32[4,256]{1,0:T(4,128)}, f32[4,256]{1,0:T(4,128)S(1)}, u32[]{:S(2)}) copy-start(f32[4,256]{1,0:T(4,128)S(1)} %get-tuple-element.28) | copy-start | bytes 12292
  101.8 4.9 %copy-start.96 = (f32[4,256]{1,0:T(4,128)}, f32[4,256]{1,0:T(4,128)S(1)}, u32[]{:S(2)}) copy-start(f32[4,256]{1,0:T(4,128)S(1)} %get-tuple-element.27) | copy-start | bytes 12292
  104.2 5.0 %copy-start.106 = (f32[1,256]{1,0:T(1,128)}, f32[1,256]{1,0:T(1,128)S(1)}, u32[]{:S(2)}) copy-start(f32[1,256]{1,0:T(1,128)S(1)} %get-tuple-element.113) | copy-start | bytes 3076
  104.2 8.8 %copy-start.117 = (f32[1,256]{1,0:T(1,128)}, f32[1,256]{1,0:T(1,128)S(1)}, u32[]{:S(2)}) copy-start(f32[1,256]{1,0:T(1,128)S(1)} %get-tuple-element.111) | copy-start | bytes 3076
  104.2 11.4 %copy-start.126 = (f32[1,256]{1,0:T(1,128)}, f32[1,256]{1,0:T(1,128)S(1)}, u32[]{:S(2)}) copy-start(f32[1,256]{1,0:T(1,128)S(1)} %get-tuple-element.110) | copy-start | bytes 3076
  104.2 13.8 %copy-start.112 = (f32[1,256]{1,0:T(1,128)}, f32[1,256]{1,0:T(1,128)S(1)}, u32[]{:S(2)}) copy-start(f32[1,256]{1,0:T(1,128)S(1)} %get-tuple-element.112) | copy-start | bytes 3076
  106.6 6.4 %copy-start.119 = (f32[1,256]{1,0:T(1,128)}, f32[1,256]{1,0:T(1,128)S(1)}, u32[]{:S(2)}) copy-start(f32[1,256]{1,0:T(1,128)S(1)} %get-tuple-element.107) | copy-start | bytes 3076
  106.6 9.0 %copy-start.128 = (f32[1,256]{1,0:T(1,128)}, f32[1,256]{1,0:T(1,128)S(1)}, u32[]{:S(2)}) copy-start(f32[1,256]{1,0:T(1,128)S(1)} %get-tuple-element.106) | copy-start | bytes 3076
  106.6 11.4 %copy-start.114 = (f32[1,256]{1,0:T(1,128)}, f32[1,256]{1,0:T(1,128)S(1)}, u32[]{:S(2)}) copy-start(f32[1,256]{1,0:T(1,128)S(1)} %get-tuple-element.108) | copy-start | bytes 3076
  125.3 53.1 %copy-start.71 = (bf16[3,3,256]{2,1,0:T(4,128)(2,1)S(1)}, bf16[3,3,256]{2,1,0:T(4,128)(2,1)}, u32[]{:S(2)}) copy-start(bf16[3,3,256]{2,1,0:T(4,128)(2,1)} %get-tuple-element.90) | copy-start | bytes 13828
  175.6 53.1 %collective-permute-start = (f32[3,3,256,256]{3,2,1,0:T(8,128)}, f32[3,3,256,256]{3,2,1,0:T(8,128)}, u32[]{:S(2)}, u32[]{:S(2)}) collective-permute-start(f32[3,3,256,256]{3,2,1,0:T(8,128)} %all-reduce.14.cloned.1.call-done), channel_id=1, source_target_pairs={{0,4},{4,0},{8,12},{12,8},{16,20},{20,16},{24,28},{28,24},{1,5},{5... | collective-permute-start | bytes 7077896 | tf_op jit(solution)/shard_map/ppermute | solution.py:90
  184.1 44.6 %copy-start.2 = (f32[3,3,256,256]{3,2,1,0:T(8,128)S(1)}, f32[3,3,256,256]{3,2,1,0:T(8,128)}, u32[]{:S(2)}) copy-start(f32[3,3,256,256]{3,2,1,0:T(8,128)} %all-reduce.14.cloned.1.call-done) | copy-start | bytes 7077892
  185.0 48.5 %copy-start.31 = (f32[9,256]{1,0:T(8,128)S(1)}, f32[9,256]{1,0:T(8,128)}, u32[]{:S(2)}) copy-start(f32[9,256]{1,0:T(8,128)} %convolution_add_fusion.49) | copy-start | bytes 27652
  185.1 49.2 %copy-start.21 = (f32[36,256]{1,0:T(8,128)S(1)}, f32[36,256]{1,0:T(8,128)}, u32[]{:S(2)}) copy-start(f32[36,256]{1,0:T(8,128)} %convolution_add_fusion.32) | copy-start | bytes 110596
  232.0 52.2 %collective-permute-start.1 = (f32[3,3,256,256]{3,2,1,0:T(8,128)}, f32[3,3,256,256]{3,2,1,0:T(8,128)}, u32[]{:S(2)}, u32[]{:S(2)}) collective-permute-start(f32[3,3,256,256]{3,2,1,0:T(8,128)} %add.721), channel_id=1, source_target_pairs={{0,8},{4,12},{8,0},{12,4},{16,24},{20,28},{24,16},{28,20},{1,9},{5... | collective-permute-start | bytes 7077896 | tf_op jit(solution)/shard_map/ppermute | solution.py:90
  235.5 3.0 copy-start.44
  235.5 3.0 copy-start.50
  235.5 3.0 copy-start.53
  235.5 3.0 copy-start.90
  235.5 3.0 copy-start.105
  235.5 3.0 copy-start.107
  235.6 3.0 copy-start.109
  239.3 50.1 %copy-start.6 = (f32[1,12,12,256]{3,2,1,0:T(8,128)S(1)}, f32[1,12,12,256]{3,2,1,0:T(8,128)}, u32[]{:S(2)}) copy-start(f32[1,12,12,256]{3,2,1,0:T(8,128)} %reshape.1115) | copy-start | bytes 442372
  239.3 50.1 %copy-start.57 = (f32[1,256]{1,0:T(1,128)S(1)}, f32[1,256]{1,0:T(1,128)}, u32[]{:S(2)}) copy-start(f32[1,256]{1,0:T(1,128)} %copy-done.54) | copy-start | bytes 3076
  239.3 50.1 %copy-start.64 = (f32[1,256]{1,0:T(1,128)S(1)}, f32[1,256]{1,0:T(1,128)}, u32[]{:S(2)}) copy-start(f32[1,256]{1,0:T(1,128)} %copy-done.61) | copy-start | bytes 3076
  239.3 50.1 %copy-start.79 = (f32[256]{0:T(256)S(1)}, f32[256]{0:T(256)}, u32[]{:S(2)}) copy-start(f32[256]{0:T(256)} %copy-done.76) | copy-start | bytes 3076
  239.3 50.1 %copy-start.86 = (f32[1,256]{1,0:T(1,128)S(1)}, f32[1,256]{1,0:T(1,128)}, u32[]{:S(2)}) copy-start(f32[1,256]{1,0:T(1,128)} %copy-done.83) | copy-start | bytes 3076
  286.9 102.5 %collective-permute-start.2 = (f32[3,3,256,256]{3,2,1,0:T(8,128)S(1)}, f32[3,3,256,256]{3,2,1,0:T(8,128)S(1)}, u32[]{:S(2)}, u32[]{:S(2)}) collective-permute-start(f32[3,3,256,256]{3,2,1,0:T(8,128)S(1)} %add.722), channel_id=1, source_target_pairs={{0,16},{4,20},{8,24},{12,28},{16,0},{20,4},{24,8},{28,12},{1,17},{... | collective-permute-start | bytes 7077896 | tf_op jit(solution)/shard_map/ppermute | solution.py:90
  (75 other events, 130.8 us)
Sparse Core Ops, SparseCore 0:
  122.0 53.5 all-reduce.13
